TPU v7x, 256 devices: a whole 4x4x8 slice. The times are simulated.
256 devices in a mesh: dom: 16 (over z_lo, y, core), rep: 16 (over x, z_hi).
Axes of the slice: x: 4, y: 4, z: 8 (z_hi: 4, z_lo: 2; z = z_hi * 2 + z_lo), core: 2. Of those that a mesh axis runs over, the one named last changes fastest.
Arguments:
- facts: float32 [1048576, 256], P(('dom', 'rep')), may hold values from -6 to 6
- row_owner: int32 [1048576, 1], P(('dom', 'rep')), may hold values from 0 to 15; in each aligned block of 4096 rows (0 to 4095, 4096 to 8191, ...) at most 512 rows name the same one
- key_offset: int32 [1048576], P(('dom', 'rep')), may hold values from 0 to 255
Outputs:
- key_means: float32 [4096, 256], P(('dom', 'rep'))
- key_counts: float32 [4096], P(('dom', 'rep'))
Inputs may be any that keep to these rules, and one draw needn't show every extreme that they name: `row_owner`: in the rows of one device no key range is named by more than 512 rows, a bound that some block reaches.
All inputs are finite; a program needn't handle non-finite values.
Results may differ from a plain program's by a relative error of at most 0.0003.
Values sent between devices are 32-bit elements; how exact they have to be, the bound alone decides.
A program may use at most 64 MiB of HBM per device.

v0:
```python
import math

import jax
import jax.numpy as jnp
from jax import lax
from jax.sharding import PartitionSpec as P

KEYS = 4096


def sent_together(arrays, axis, dim, along):
    widths = [math.prod(a.shape[along:]) for a in arrays]
    both = jnp.concatenate(
        [a.reshape(*a.shape[:along], w) for a, w in zip(arrays, widths)], axis=along
    )
    result = lax.psum_scatter(both, axis, scatter_dimension=dim, tiled=True)
    pieces = jnp.split(result, [sum(widths[:k]) for k in range(1, len(widths))], axis=along)
    return tuple(
        (b.reshape(*result.shape[:along], *a.shape[along:]) for a, b in zip(arrays, pieces))
    )


def in_blocks(x, dim, size):
    shape = x.shape
    pieces = x.reshape(*shape[:dim], size, shape[dim] // size, *shape[dim + 1 :])
    return jnp.moveaxis(pieces, dim, 0)


def sent_and_summed(x, axis, dim):
    pieces = in_blocks(x, dim, lax.axis_size(axis))
    arrived = lax.all_to_all(pieces, axis, split_axis=0, concat_axis=0, tiled=True)
    return arrived.sum(axis=0)


def in_one_piece(arrays, axis, dim, along):
    columns = [a.reshape(*a.shape[:along], -1) for a in arrays]
    both = jnp.concatenate(columns, axis=along)
    result, at, gathered = (sent_and_summed(both, axis, dim), 0, [])
    for a, column in zip(arrays, columns):
        share = result[..., at : at + column.shape[along]]
        gathered.append(share.reshape(*share.shape[:along], *a.shape[along:]))
        at += column.shape[along]
    return tuple(gathered)


def block_table(offsets, high_part, low_part, key_step):
    wanted = jnp.arange(key_step, dtype=jnp.int32)
    onehot = (offsets[:, :, None] == wanted[None, None, :]).astype(jnp.bfloat16)
    upper = jnp.einsum("grk,grm->gkm", onehot, high_part, preferred_element_type=jnp.float32)
    lower = jnp.einsum("grk,grm->gkm", onehot, low_part, preferred_element_type=jnp.float32)
    return (upper + lower, jnp.sum(onehot, axis=1, dtype=jnp.float32))


def grouped_table(offsets, values, key_span):
    width = values.shape[-1]
    groups = offsets.shape[0]
    high_part = lax.optimization_barrier(values.astype(jnp.bfloat16))
    low_part = (values - high_part.astype(jnp.float32)).astype(jnp.bfloat16)
    key_step = min(512, key_span)
    table_sums, table_counts = block_table(offsets, high_part, low_part, key_step)
    return (table_sums.reshape(groups * key_span, width), table_counts.reshape(groups * key_span))


def bucket_rows(row_range, n_dom, capacity):
    rows_here = row_range.shape[0]
    range_hot = (row_range[:, None] == jnp.arange(n_dom, dtype=jnp.int32)[None, :]).astype(
        jnp.int32
    )
    before = jnp.cumsum(range_hot, axis=0) - range_hot
    slot_of = jnp.sum(range_hot * before, axis=1)
    position = row_range * capacity + slot_of
    empty = jnp.full((n_dom * capacity,), rows_here, jnp.int32)
    return empty.at[position].set(
        jnp.arange(rows_here, dtype=jnp.int32), unique_indices=True, mode="drop"
    )


def finish(table_sums, table_counts):
    return (table_sums / jnp.maximum(table_counts, 1.0)[:, None], table_counts)


def per_device(facts, row_owner, key_offset):
    row_range = row_owner[:, 0]
    n_dom = lax.axis_size("dom")
    key_span = KEYS // n_dom
    capacity = 2 * facts.shape[0] // n_dom
    measures = facts.shape[1]
    source = bucket_rows(row_range, n_dom, capacity)
    picked = jnp.take(facts, source, axis=0, mode="fill", fill_value=0.0)
    offsets = jnp.take(key_offset, source, axis=0, mode="fill", fill_value=-1)
    local_sums, local_counts = grouped_table(
        offsets.reshape(n_dom, capacity), picked.reshape(n_dom, capacity, measures), key_span
    )
    range_sums, range_counts = sent_together((local_sums, local_counts), "dom", 0, 1)
    table_sums, table_counts = in_one_piece((range_sums, range_counts), "rep", 0, 1)
    return finish(table_sums, table_counts)


def solution(mesh):
    placed = (P(("dom", "rep"), None), P(("dom", "rep"), None), P(("dom", "rep")))
    return jax.shard_map(
        per_device,
        mesh=mesh,
        in_specs=placed,
        out_specs=(P(("dom", "rep"), None), P(("dom", "rep"))),
        check_vma=False,
    )
```

profile of v0, /device:TPU:2, one launch (start us, length us, event | category | flops | bytes accessed | tf_op | source)
XLA Modules:
  0.0 238.9 jit_solution(2630749423743461588)
XLA Ops:
  7.2 0.0 copy-start
  7.2 0.0 reduce-scatter.2.cloned.1.call-start
  7.2 0.7 fusion.11
  8.0 4.6 %reduce-window.6 = s32[16,32,128]{2,1,0:T(8,128)S(1)} reduce-window(s32[16,32,128]{2,1,0:T(8,128)S(1)} %fusion.11, s32[]{:T(128)} %constant.24.clone.1), window={size=1x1x128 pad=0_0x0_0x127_0}, to_apply=%region_0.0 | reduce-window | flops 8323072 | bytes 524292 | tf_op jit(solution)/shard_map/reduce-window
  12.6 0.5 slice_reduce_fusion
  13.1 0.2 reduce-window.9
  13.2 0.1 broadcast_add_fusion
  13.4 0.9 fusion.10
  14.3 0.7 compare_select_fusion
  15.1 15.5 %scatter_custom_fusion = s32[8192]{0:T(1024)S(1)} fusion(s32[4096]{0:T(1024)S(1)} %bitcast.42, s32[4096]{0:T(1024)S(1)} %iota.15, s32[]{:T(128)} %constant.22.clone.1), kind=kCustom, calls=%fused_computation.31 | custom fusion | bytes 32772 | tf_op jit(solution)/shard_map/scatter | solution.py:73
  30.7 33.6 %gather_fusion.1 = f32[8192,256]{1,0:T(8,128)} fusion(f32[4096,256]{1,0:T(8,128)} %param.3, s32[8192]{0:T(1024)S(1)} %fusion.12), kind=kCustom, calls=%fused_computation.1 | custom fusion | bytes 16809984 | tf_op jit(solution)/shard_map/jit(_take)/gather | solution.py:89
  64.3 6.3 %select_convert_fusion = bf16[16,512,256]{2,1,0:T(8,128)(2,1)} fusion(f32[16,512,256]{2,1,0:T(8,128)} %bitcast.30, pred[16,512]{1,0:T(8,128)(4,1)S(1)} %reduce_and.8), kind=kLoop, calls=%fused_computation.9 | loop fusion | flops 2097152 | bytes 12591104 | tf_op jit(solution)/shard_map/convert_element_type | solution.py:57
  70.5 0.0 copy-done
  70.5 45.5 %gather_fusion = s32[8192]{0:T(1024)S(1)} fusion(s32[4096]{0:T(1024)S(1)} %copy-done, s32[8192]{0:T(1024)S(1)} %fusion.12), kind=kCustom, calls=%fused_computation | custom fusion | bytes 98304 | tf_op jit(solution)/shard_map/jit(_take)/gather | solution.py:90
  116.1 0.9 convert_reduce_fusion
  117.0 0.0 copy-start.1
  117.0 6.9 %fusion.1 = f32[16,256,256]{2,1,0:T(8,128)S(1)} fusion(bf16[16,512,256]{2,1,0:T(8,128)(2,1)} %select_convert_fusion, f32[16,512,256]{2,1,0:T(8,128)} %bitcast.31, s32[16,512]{1,0:T(8,128)S(1)} %broadcast_select_fusion, pred[16,512]{1,0:T(8,128)(4,1)S(1)} %reduce_and.8), kind=kOutput, calls=%fused_computation.7 | convolution fusion | flops 1084227584 | bytes 16818176 | tf_op jit(solution)/shard_map/grk,grm->gkm/dot_general | solution.py:50
  123.9 0.0 copy-done.1
  124.0 3.5 %fusion.7 = f32[16,256,256]{2,1,0:T(8,128)} fusion(f32[16,256,256]{2,1,0:T(8,128)S(1)} %fusion.1, bf16[16,512,256]{2,1,0:T(8,128)(2,1)S(1)} %copy-done.1, s32[16,512]{1,0:T(8,128)S(1)} %broadcast_select_fusion), kind=kOutput, calls=%fused_computation.15 | convolution fusion | flops 1076887552 | bytes 12615680 | tf_op jit(solution)/shard_map/grk,grm->gkm/dot_general | solution.py:49
  127.5 0.6 copy.8
  128.1 5.3 %pad_maximum_fusion = f32[4096,257]{1,0:T(8,128)} fusion(f32[4096,1]{1,0:T(8,128)S(1)} %bitcast.33, f32[4096,256]{1,0:T(8,128)} %bitcast.32), kind=kLoop, calls=%fused_computation.10 | loop fusion | flops 1052672 | bytes 8421376 | tf_op jit(solution)/shard_map/concatenate | solution.py:13
  133.4 0.0 reduce-scatter.2.cloned.1.call-update
  133.4 76.9 %reduce-scatter.2.cloned.1.call-done = f32[256,257]{1,0:T(8,128)} async-done(((f32[4096,257]{1,0:T(8,128)}), f32[256,257]{1,0:T(8,128)}) %reduce-scatter.2.cloned.1.call-update) | async-done | bytes 263184 | tf_op jit(solution)/shard_map/reduce_scatter | solution.py:16
  210.3 20.4 %all_to_all.5 = f32[16,16,257]{2,1,0:T(8,128)S(1)} all-to-all(f32[16,16,257]{2,1,0:T(8,128)} %bitcast.35), channel_id=1, replica_groups=mesh['dom'=16,'rep'=16] {'rep'}, dimensions={0} | all-to-all | bytes 526336 | tf_op jit(solution)/shard_map/all_to_all | solution.py:31
  230.7 0.6 slice_reduce_fusion.1
  231.4 0.7 slice_divide_fusion
  (8 shorter events, 0.1 us)
Async XLA Ops:
  7.2 63.4 %copy-start = (s32[4096]{0:T(1024)S(1)}, s32[4096]{0:T(1024)}, u32[]{:S(2)}) copy-start(s32[4096]{0:T(1024)} %param.5) | copy-start | bytes 49156
  7.2 203.1 %reduce-scatter.2.cloned.1.call-start = ((), (), s32[]{:S(2)}) async-start(), calls=%async_computation.2 | async-start | bytes 6684672 | tf_op jit(solution)/shard_map/reduce_scatter | solution.py:16
  117.0 6.9 %copy-start.1 = (bf16[16,512,256]{2,1,0:T(8,128)(2,1)S(1)}, bf16[16,512,256]{2,1,0:T(8,128)(2,1)}, u32[]{:S(2)}) copy-start(bf16[16,512,256]{2,1,0:T(8,128)(2,1)} %select_convert_fusion) | copy-start | bytes 12582916
Sparse Core Ops, SparseCore 0:
  133.5 76.7 reduce-scatter.1
where the time goes:
time: 241 us; the launch traced here: 239 us
  local copies, waits for them, and re-layouts  95.8 us (40%)
  waiting for transfers between devices  76.9 us (32%)
  other arithmetic  21.2 us (9%)
  blocking collectives  20.4 us (8%)
  between operations  14.2 us (6%)
  matrix products  10.4 us (4%)
    reduce_scatter x1, waiting for transfers between devices, sent_together(): result = lax.psum_scatter(both, axis, scatter_dimension=dim, tiled=True)  76.9 us
    gather x2, local copies, waits for them, and re-layouts, per_device(): offsets = jnp.take(key_offset, source, axis=0, mode='fill', fill_value=-1)  45.5 us
    gather x1, local copies, waits for them, and re-layouts, per_device(): picked = jnp.take(facts, source, axis=0, mode='fill', fill_value=0.0)  33.6 us
    all_to_all x1, blocking collectives, sent_and_summed(): lax.all_to_all(pieces, axis, split_axis=0, concat_axis=0, tiled=True)  20.4 us
    scatter x1, local copies, waits for them, and re-layouts, bucket_rows(): empty.at[position]  15.5 us
    dot_general x1, matrix products, block_table(): jnp.einsum('grk,grm->gkm', onehot, low_part, preferred_element_type=jnp.f...  6.9 us
    convert_element_type x1, other arithmetic, grouped_table(): high_part = lax.optimization_barrier(values.astype(jnp.bfloat16))  6.28 us
    concatenate x1, other arithmetic, sent_together(): jnp.concatenate([a.reshape(*a.shape[:along], w) for a, w in zip(arrays, w...  5.26 us
  transfers between devices with their start and end apart: 1, of which 1 were waited for; matrix products, arithmetic and copies ran while one was open for 0% of the time, Pallas kernels for 0%

commit v1 on v0

v1 whole, which is shorter than its diff:
```python
import functools

import jax
import jax.numpy as jnp
from jax import lax
from jax.experimental import pallas as pl
from jax.experimental.pallas import tpu as pltpu
from jax.sharding import PartitionSpec as P

MESH = pl.DeviceIdType.MESH
ROWS = 4096
KEYS = 4096
M = 256
UNITS = 8
F32 = jnp.float32
BF16 = jnp.bfloat16


def when(cond, fn):
    if isinstance(cond, (bool, int)):
        if cond:
            fn()
    else:
        pl.when(cond)(fn)


def rows(start, size):
    return pl.ds(pl.multiple_of(start, size), size)


def kernel(
    ids_ref, facts_ref, means_ref, counts_ref,
    fbuf, hl, own, part, land, xa, xb, ya, yb, yr, yxa, yxb, xr, xya, xyb, fin, zl_buf,
    cnt, cland, czland,
    f_sem, d_s, d_r, xa_s, xa_r, xb_s, xb_r, ya_s, ya_r, yb_s, yb_r,
    yxa_s, yxa_r, yxb_s, yxb_r, xya_s, xya_r, xyb_s, xyb_r, z_s, z_r, c_s, c_r, cz_s, cz_r,
):
    dom, rep = lax.axis_index("dom"), lax.axis_index("rep")
    z_lo, y, core = dom // 8, (dom // 2) % 4, dom % 2
    x, z_hi = rep // 4, rep % 4

    def at(zl=z_lo, yy=y, cc=core, xx=x, zh=z_hi):
        return {"dom": zl * 8 + yy * 2 + cc, "rep": xx * 4 + zh}

    partner = at(cc=1 - core)
    xp, xm = at(xx=(x + 1) % 4), at(xx=(x + 3) % 4)
    yp, ym = at(yy=(y + 1) % 4), at(yy=(y + 3) % 4)

    def z_peer(k):
        z = (z_hi * 2 + z_lo + k) % 8
        return z // 2, z % 2

    peers = [partner, xp, xm, yp, ym]
    for k in range(1, 8):
        zh, zl = z_peer(k)
        peers.append(at(zl=zl, zh=zh))

    barrier = pltpu.get_barrier_semaphore()
    for p in peers:
        pl.semaphore_signal(barrier, inc=1, device_id=p, device_id_type=MESH)

    def rc(src, dst, ss, rs, dev):
        return pltpu.make_async_remote_copy(
            src_ref=src, dst_ref=dst, send_sem=ss, recv_sem=rs, device_id=dev, device_id_type=MESH
        )

    def arrived(buf, ss, rs):
        rc(buf, buf, ss, rs, partner).wait_recv()

    def sent(buf, ss, rs):
        rc(buf, buf, ss, rs, partner).wait_send()

    def f_copy(i):
        s = pl.ds(i * 512, 512)
        return pltpu.make_async_copy(facts_ref.at[s, :], fbuf.at[s, :], f_sem.at[i])

    for i in range(8):
        f_copy(i).start()

    ids = ids_ref[...]
    owner_hot = (lax.broadcasted_iota(jnp.int32, (16, ROWS), 0) == (ids >> 8)).astype(F32).astype(BF16)
    off_hot = (lax.broadcasted_iota(jnp.int32, (256, ROWS), 0) == (ids & 255)).astype(F32).astype(BF16)
    cnt[0] = lax.dot_general(owner_hot, off_hot, (((1,), (1,)), ((), ())), preferred_element_type=F32)

    pl.semaphore_wait(barrier, len(peers))

    def c_send(k, dev):
        rc(cnt.at[k], cland.at[k], c_s.at[k], c_r.at[k], dev).start()

    def c_take(k):
        arrived(cland.at[k], c_s.at[k], c_r.at[k])
        cnt[k + 1] = cnt[k] + cland[k]

    c_send(0, partner)

    for i in range(8):
        f_copy(i).wait()

        def split(j, c, i=i):
            s = rows(i * 512 + j * 128, 128)
            v = fbuf[s, :]
            h = v.astype(BF16)
            hl[s, 0:256] = h
            hl[s, 256:512] = (v - h.astype(F32)).astype(BF16)
            return c

        lax.fori_loop(0, 4, split, 0)

    x_even, y_even = x % 2 == 0, y % 2 == 0

    def pick(even, a, b):
        return {n: jnp.where(even, a[n], b[n]) for n in a}

    def count_step(k):
        c_take(k - 1)
        dev = (
            pick(x_even, xp, xm), pick(x_even, xm, xp), pick(y_even, yp, ym), pick(y_even, ym, yp)
        )[k - 1]
        c_send(k, dev)

    def count_z():
        c_take(4)
        for k in range(1, 8):
            zh, zl = z_peer(k)
            rc(cnt.at[5], czland.at[k - 1], cz_s.at[k - 1], cz_r.at[k - 1], at(zl=zl, zh=zh)).start()

    flipped = jnp.bitwise_xor(ids, core * 256)

    def compute(t, p, q):
        rel = jnp.where(q == 0, 2, jnp.where(q == 1, 1, jnp.where(q == 2, 3, 0)))
        zl = (z_lo + p) % 2
        base = (zl * 4 + (y + rel) % 4) * 512
        hot = (lax.broadcasted_iota(jnp.int32, (512, ROWS), 0) == (flipped - base)).astype(F32).astype(BF16)
        acc = jnp.dot(hot, hl[...], preferred_element_type=F32)
        own[t, 0] = acc[0:256, 0:128] + acc[0:256, 256:384]
        own[t, 1] = acc[0:256, 128:256] + acc[0:256, 384:512]
        part[t, 0] = acc[256:512, 0:128] + acc[256:512, 256:384]
        part[t, 1] = acc[256:512, 128:256] + acc[256:512, 384:512]
        rc(part.at[t], land.at[t], d_s.at[t], d_r.at[t], partner).start()

    def ring_x_a(buf, la, s, r):
        far = ((x + 2) % 4) * 64
        rc(buf.at[rows(far, 32), :], la.at[0], s.at[0], r.at[0], xp).start()
        rc(buf.at[rows(far + 32, 32), :], la.at[1], s.at[1], r.at[1], xm).start()

    def ring_x_b(buf, la, lb, sa, ra, sb, rb):
        nxt, prv = ((x + 1) % 4) * 64, ((x + 3) % 4) * 64
        arrived(la.at[0], sa.at[0], ra.at[0])
        s = rows(nxt, 32)
        buf[s, :] = buf[s, :] + la[0]
        rc(buf.at[rows(nxt, 64), :], lb.at[0], sb.at[0], rb.at[0], xp).start()
        arrived(la.at[1], sa.at[1], ra.at[1])
        s = rows(prv + 32, 32)
        buf[s, :] = buf[s, :] + la[1]
        rc(buf.at[rows(prv, 64), :], lb.at[1], sb.at[1], rb.at[1], xm).start()

    def ring_x_c(buf, lb, sb, rb):
        arrived(lb.at[0], sb.at[0], rb.at[0])
        arrived(lb.at[1], sb.at[1], rb.at[1])
        return buf[rows(x * 64, 64), :] + lb[0] + lb[1]

    def ring_y(buf, half, q, la, lb, sa, ra, sb, rb, done):
        lo, hi = pl.ds(0, half), pl.ds(half, half)

        def far():
            rc(buf.at[lo, :], la.at[0], sa.at[0], ra.at[0], yp).start()
            rc(buf.at[hi, :], la.at[1], sa.at[1], ra.at[1], ym).start()

        def nxt():
            arrived(la.at[0], sa.at[0], ra.at[0])
            buf[lo, :] = buf[lo, :] + la[0]
            rc(buf, lb.at[0], sb.at[0], rb.at[0], yp).start()

        def prv():
            arrived(la.at[1], sa.at[1], ra.at[1])
            buf[hi, :] = buf[hi, :] + la[1]
            rc(buf, lb.at[1], sb.at[1], rb.at[1], ym).start()

        def home():
            arrived(lb.at[0], sb.at[0], rb.at[0])
            arrived(lb.at[1], sb.at[1], rb.at[1])
            done(buf[...] + lb[0] + lb[1])

        for k, fn in enumerate((far, nxt, prv, home)):
            when(q == k, fn)

    def stage1(t, p, q):
        arrived(land.at[t], d_s.at[t], d_r.at[t])
        own[t, 0] = own[t, 0] + land[t, 0]
        ring_x_a(own.at[t, 0], xa.at[t], xa_s.at[t], xa_r.at[t])
        own[t, 1] = own[t, 1] + land[t, 1]

        def done(v):
            yr[p] = v
            ring_x_a(yr.at[p], yxa.at[p], yxa_s.at[p], yxa_r.at[p])

        ring_y(
            own.at[t, 1], 128, q, ya.at[p], yb.at[p], ya_s.at[p], ya_r.at[p], yb_s.at[p], yb_r.at[p], done
        )

    def stage2(t, p, q):
        ring_x_b(own.at[t, 0], xa.at[t], xb.at[t], xa_s.at[t], xa_r.at[t], xb_s.at[t], xb_r.at[t])

        def tail():
            ring_x_b(yr.at[p], yxa.at[p], yxb.at[p], yxa_s.at[p], yxa_r.at[p], yxb_s.at[p], yxb_r.at[p])

        when(q == 3, tail)

    my_z = z_hi * 2 + z_lo

    def stage3(t, p, q):
        xr[t] = ring_x_c(own.at[t, 0], xb.at[t], xb_s.at[t], xb_r.at[t])

        def done(v):
            fin[p, 0] = v
            fin[p, 1] = ring_x_c(yr.at[p], yxb.at[p], yxb_s.at[p], yxb_r.at[p])
            zl = (z_lo + p) % 2
            for k in range(4):
                zh = (z_hi + k) % 4

                def send(zh=zh, k=k):
                    rc(
                        fin.at[p, :, rows(zh * 16, 16), :], zl_buf.at[my_z], z_s.at[p * 4 + k],
                        z_r.at[my_z], at(zl=zl, zh=zh),
                    ).start()

                when((p == 1) if k == 0 else True, send)

        ring_y(
            xr.at[t], 32, q, xya.at[p], xyb.at[p], xya_s.at[p], xya_r.at[p], xyb_s.at[p], xyb_r.at[p], done
        )

    def step(t, c):
        for lag, stage in ((3, stage3), (2, stage2), (1, stage1)):

            def go(lag=lag, stage=stage):
                o = t - lag
                stage(o, o // 4, o % 4)

            when(t >= lag, go)
        for k in range(1, 5):
            when(t == k, functools.partial(count_step, k))
        when(t == 5, count_z)
        compute(t, t // 4, t % 4)
        return c

    lax.fori_loop(0, UNITS, step, 0)

    stage3(5, 1, 1)
    stage2(6, 1, 2)
    stage1(7, 1, 3)
    stage3(6, 1, 2)

    total = cnt[5]
    for k in range(7):
        arrived(czland.at[k], cz_s.at[k], cz_r.at[k])
        total = total + czland[k]
    row = jnp.sum(
        jnp.where(lax.broadcasted_iota(jnp.int32, (16, 256), 0) == dom, total, 0.0), axis=0, keepdims=True
    )
    mine = lax.broadcasted_iota(jnp.int32, (16, 256), 1) == (
        lax.broadcasted_iota(jnp.int32, (16, 256), 0) + rep * 16
    )
    column = jnp.sum(jnp.where(mine, row, 0.0), axis=1, keepdims=True)
    eye = lax.broadcasted_iota(jnp.int32, (16, 16), 0) == lax.broadcasted_iota(jnp.int32, (16, 16), 1)
    counts_ref[...] = jnp.sum(jnp.where(eye, column, 0.0), axis=0, keepdims=True)
    divisor = jnp.maximum(column, 1.0)

    stage2(7, 1, 3)
    stage3(7, 1, 3)

    mine_rows = rows(z_hi * 16, 16)
    left, right = fin[0, 0, mine_rows, :], fin[0, 1, mine_rows, :]
    for k in range(1, 8):
        zh, zl = z_peer(k)
        z = zh * 2 + zl
        arrived(zl_buf.at[z], z_s.at[0], z_r.at[z])
        left = left + zl_buf[z, 0]
        right = right + zl_buf[z, 1]
    means_ref[:, 0:128] = left / divisor
    means_ref[:, 128:256] = right / divisor

    def drain(t, c):
        sent(part.at[t], d_s.at[t], d_r.at[t])
        for k in range(2):
            sent(xa.at[t, k], xa_s.at[t, k], xa_r.at[t, k])
            sent(xb.at[t, k], xb_s.at[t, k], xb_r.at[t, k])
        return c

    lax.fori_loop(0, UNITS, drain, 0)
    for p in range(2):
        for k in range(2):
            for buf, s, r in (
                (ya, ya_s, ya_r), (yb, yb_s, yb_r), (yxa, yxa_s, yxa_r), (yxb, yxb_s, yxb_r),
                (xya, xya_s, xya_r), (xyb, xyb_s, xyb_r),
            ):
                sent(buf.at[p, k], s.at[p, k], r.at[p, k])
    for k in range(1, 8):
        sent(zl_buf.at[0], z_s.at[k], z_r.at[0])
    for k in range(5):
        sent(cland.at[k], c_s.at[k], c_r.at[k])
    for k in range(7):
        sent(czland.at[k], cz_s.at[k], cz_r.at[k])


def per_device(facts, row_owner, key_offset):
    ids = (row_owner[:, 0] * 256 + key_offset).reshape(1, ROWS)
    dma = pltpu.SemaphoreType.DMA
    vm = pltpu.VMEM
    means, counts = pl.pallas_call(
        kernel,
        out_shape=(jax.ShapeDtypeStruct((16, M), F32), jax.ShapeDtypeStruct((1, 16), F32)),
        in_specs=[pl.BlockSpec(memory_space=pltpu.VMEM), pl.BlockSpec(memory_space=pl.ANY)],
        out_specs=(pl.BlockSpec(memory_space=pltpu.VMEM), pl.BlockSpec(memory_space=pltpu.VMEM)),
        scratch_shapes=[
            vm((ROWS, M), F32), vm((ROWS, 2 * M), BF16),
            vm((8, 2, 256, 128), F32), vm((8, 2, 256, 128), F32), vm((8, 2, 256, 128), F32),
            vm((8, 2, 32, 128), F32), vm((8, 2, 64, 128), F32),
            vm((2, 2, 128, 128), F32), vm((2, 2, 256, 128), F32), vm((2, 256, 128), F32),
            vm((2, 2, 32, 128), F32), vm((2, 2, 64, 128), F32), vm((8, 64, 128), F32),
            vm((2, 2, 32, 128), F32), vm((2, 2, 64, 128), F32), vm((2, 2, 64, 128), F32),
            vm((8, 2, 16, 128), F32),
            vm((6, 16, 256), F32), vm((5, 16, 256), F32), vm((7, 16, 256), F32),
            dma((8,)), dma((8,)), dma((8,)),
            dma((8, 2)), dma((8, 2)), dma((8, 2)), dma((8, 2)),
            dma((2, 2)), dma((2, 2)), dma((2, 2)), dma((2, 2)),
            dma((2, 2)), dma((2, 2)), dma((2, 2)), dma((2, 2)),
            dma((2, 2)), dma((2, 2)), dma((2, 2)), dma((2, 2)),
            dma((8,)), dma((8,)), dma((5,)), dma((5,)), dma((7,)), dma((7,)),
        ],
        compiler_params=pltpu.CompilerParams(
            collective_id=0, has_side_effects=True, vmem_limit_bytes=56 * 1024 * 1024
        ),
    )(ids, facts)
    return means, counts.reshape(16)


def solution(mesh):
    placed = (P(("dom", "rep"), None), P(("dom", "rep"), None), P(("dom", "rep")))
    return jax.shard_map(
        per_device,
        mesh=mesh,
        in_specs=placed,
        out_specs=(P(("dom", "rep"), None), P(("dom", "rep"))),
        check_vma=False,
    )
```

time: 241 us -> 61.3 us (0.25)
  local copies, waits for them, and re-layouts: 95.8 us -> 2.46 us
  waiting for transfers between devices: 76.9 us -> 0 us
  Pallas kernels: 0 us -> 55.2 us
  blocking collectives: 20.4 us -> 0 us
  other arithmetic: 21.2 us -> 2.06 us
  between operations: 14.2 us -> 0.64 us
  matrix products: 10.4 us -> 0 us
    gather x3 -> x0, local copies, waits for them, and re-layouts: 79.1 us -> none  [the longest x2 45.5 us: per_device(): offsets = jnp.take(key_offset, source, axis=0, mode='fill', fill_value=-1)]
    reduce_scatter x1 -> x0, waiting for transfers between devices: 76.9 us -> none  [sent_together(): result = lax.psum_scatter(both, axis, scatter_dimension=dim, tiled=True)]
    pallas_call x0 -> x1, Pallas kernels: none -> 55.2 us  [per_device(): pl.pallas_call(kernel, out_shape=(jax.ShapeDtypeStruct((16, M), F32), jax...]
    all_to_all x1 -> x0, blocking collectives: 20.4 us -> none  [sent_and_summed(): lax.all_to_all(pieces, axis, split_axis=0, concat_axis=0, tiled=True)]
    scatter x1 -> x0, local copies, waits for them, and re-layouts: 15.5 us -> none  [bucket_rows(): empty.at[position]]
    dot_general x2 -> x0, matrix products: 10.4 us -> none  [the longest x1 6.9 us: block_table(): jnp.einsum('grk,grm->gkm', onehot, low_part, preferred_element_type=jnp.f...]
    convert_element_type x2 -> x0, other arithmetic: 7.02 us -> none  [the longest x1 6.28 us: grouped_table(): high_part = lax.optimization_barrier(values.astype(jnp.bfloat16))]
    concatenate x1 -> x0, other arithmetic: 5.26 us -> none  [sent_together(): jnp.concatenate([a.reshape(*a.shape[:along], w) for a, w in zip(arrays, w...]
  transfers between devices with their start and end apart: 1 -> 0, of which waited for: 1 -> 0; matrix products, arithmetic and copies ran while one was open for 0% -> 0% of each run, Pallas kernels for 0% -> 0%
where the time goes in v1:
time: 61.3 us; the launch traced here: 60.4 us
  Pallas kernels  55.2 us (90%)
  local copies, waits for them, and re-layouts  2.46 us (4%)
  other arithmetic  2.06 us (3%)
  between operations  0.64 us (1%)
    pallas_call x1, Pallas kernels, per_device(): pl.pallas_call(kernel, out_shape=(jax.ShapeDtypeStruct((16, M), F32), jax...  55.2 us
    unnamed x2, local copies, waits for them, and re-layouts  2.46 us
    add x1, other arithmetic, per_device(): ids = (row_owner[:, 0] * 256 + key_offset).reshape(1, ROWS)  1.33 us

profile of v1, /device:TPU:2, one launch (start us, length us, event | category | flops | bytes accessed | tf_op | source)
XLA Modules:
  0.0 60.4 jit_solution(6809246039545335732)
XLA Ops:
  0.6 0.7 %broadcast_multiply_fusion = s32[4096,1]{0,1:T(1,128)S(1)} fusion(s32[4096,1]{0,1:T(1,128)} %param.4), kind=kLoop, calls=%fused_computation | loop fusion | flops 4096 | bytes 32768 | tf_op jit(solution)/shard_map/mul | solution.py:307
  1.4 1.3 %add.3 = s32[4096]{0:T(1024)} add(s32[4096]{0:T(1024)S(1)} %bitcast.4, s32[4096]{0:T(1024)} %param.5) | non-fusion elementwise | flops 4096 | bytes 49152 | tf_op jit(solution)/shard_map/add | solution.py:307
  2.7 55.2 %shard_map.50 = (f32[16,256]{1,0:T(8,128)}, f32[1,16]{1,0:T(1,128)}) custom-call(s32[1,4096]{1,0:T(1,128)} %bitcast.3, f32[4096,256]{1,0:T(8,128)} %facts_ref.1), custom_call_target="tpu_custom_call" | custom-call | tf_op jit(solution)/shard_map/pallas_call | solution.py:310
  57.9 1.3 %copy.7 = f32[16,256]{1,0:T(8,128)} copy(f32[16,256]{1,0:T(8,128)} %get-tuple-element.8) | data formatting | bytes 32768
  59.3 1.1 %copy.8 = f32[16]{0:T(128)} copy(f32[16]{0:T(128)} %bitcast.5) | data formatting | bytes 128

commit v2 on v1

v2 whole, which is shorter than its diff:
```python
import jax
import jax.numpy as jnp
from jax import lax
from jax.experimental import pallas as pl
from jax.experimental.pallas import tpu as pltpu
from jax.sharding import PartitionSpec as P

MESH = pl.DeviceIdType.MESH
ROWS = 4096
KEYS = 4096
M = 256
UNITS = 8
F32 = jnp.float32
BF16 = jnp.bfloat16


def when(cond, fn):
    if isinstance(cond, (bool, int)):
        if cond:
            fn()
    else:
        pl.when(cond)(fn)


def rows(start, size):
    return pl.ds(pl.multiple_of(start, size), size)


def kernel(
    owner_ref, offset_ref, facts_ref, out_ref,
    ownbuf, offbuf, fbuf, hl, own, part, land, xa, xb, ya, yb, yr, yxa, yxb, xr, xya, xyb, fin, zl_buf,
    cnt, cnt_x, cnt_y, cx, cy, cz,
    i_sem, f_sem, d_s, d_r, xa_s, xa_r, xb_s, xb_r, ya_s, ya_r, yb_s, yb_r,
    yxa_s, yxa_r, yxb_s, yxb_r, xya_s, xya_r, xyb_s, xyb_r, z_s, z_r, cx_s, cx_r, cy_s, cy_r, cz_s, cz_r,
):
    dom, rep = lax.axis_index("dom"), lax.axis_index("rep")
    z_lo, y, core = dom // 8, (dom // 2) % 4, dom % 2
    x, z_hi = rep // 4, rep % 4

    def at(zl=z_lo, yy=y, cc=core, xx=x, zh=z_hi):
        return {"dom": zl * 8 + yy * 2 + cc, "rep": xx * 4 + zh}

    partner = at(cc=1 - core)
    xp, xm = at(xx=(x + 1) % 4), at(xx=(x + 3) % 4)
    yp, ym = at(yy=(y + 1) % 4), at(yy=(y + 3) % 4)

    def z_peer(k):
        z = (z_hi * 2 + z_lo + k) % 8
        return z // 2, z % 2

    peers = [partner]
    for k in range(1, 4):
        peers += [at(xx=(x + k) % 4), at(cc=1 - core, xx=(x + k) % 4), at(yy=(y + k) % 4)]
    for k in range(1, 8):
        zh, zl = z_peer(k)
        peers.append(at(zl=zl, zh=zh))

    barrier = pltpu.get_barrier_semaphore()
    for p in peers:
        pl.semaphore_signal(barrier, inc=1, device_id=p, device_id_type=MESH)

    def rc(src, dst, ss, rs, dev):
        return pltpu.make_async_remote_copy(
            src_ref=src, dst_ref=dst, send_sem=ss, recv_sem=rs, device_id=dev, device_id_type=MESH
        )

    def arrived(buf, ss, rs):
        rc(buf, buf, ss, rs, partner).wait_recv()

    def sent(buf, ss):
        rc(buf, buf, ss, d_r.at[0], partner).wait_send()

    def f_copy(i):
        s = pl.ds(i * 512, 512)
        return pltpu.make_async_copy(facts_ref.at[s, :], fbuf.at[s, :], f_sem.at[i])

    i_copies = (
        pltpu.make_async_copy(owner_ref, ownbuf, i_sem.at[0]),
        pltpu.make_async_copy(offset_ref, offbuf, i_sem.at[1]),
    )
    for c in i_copies:
        c.start()
    for i in range(8):
        f_copy(i).start()
    for c in i_copies:
        c.wait()

    owner, offset = ownbuf[...], offbuf[...]
    owner_hot = (lax.broadcasted_iota(jnp.int32, (16, ROWS), 0) == (owner % 2) * 8 + owner // 2).astype(F32).astype(BF16)
    off_hot = (lax.broadcasted_iota(jnp.int32, (256, ROWS), 0) == offset).astype(F32).astype(BF16)
    counts = lax.dot_general(owner_hot, off_hot, (((1,), (1,)), ((), ())), preferred_element_type=F32)
    cnt[0], cnt[1] = counts[0:8], counts[8:16]

    def count_x():
        for k in range(1, 8):
            cc, xx = (core + k // 4) % 2, (x + k) % 4
            rc(cnt.at[cc], cx.at[k - 1], cx_s, cx_r.at[k - 1], at(cc=cc, xx=xx)).start()

    def count_y():
        total = cnt[core]
        for k in range(7):
            arrived(cx.at[k], cx_s, cx_r.at[k])
            total = total + cx[k]
        cnt_x[...] = total
        for k in range(1, 4):
            rc(cnt_x, cy.at[k - 1], cy_s, cy_r.at[k - 1], at(yy=(y + k) % 4)).start()

    def count_z():
        total = cnt_x[...]
        for k in range(3):
            arrived(cy.at[k], cy_s, cy_r.at[k])
            total = total + cy[k]
        cnt_y[...] = total
        for k in range(1, 8):
            zh, zl = z_peer(k)
            rc(cnt_y, cz.at[k - 1], cz_s, cz_r.at[k - 1], at(zl=zl, zh=zh)).start()

    for i in range(8):
        f_copy(i).wait()

        def split(j, c, i=i):
            s = rows(i * 512 + j * 128, 128)
            v = fbuf[s, :]
            h = v.astype(BF16)
            hl[s, 0:256] = h
            hl[s, 256:512] = (v - h.astype(F32)).astype(BF16)
            return c

        lax.fori_loop(0, 4, split, 0)

    flipped = jnp.bitwise_xor(owner, core) * 256 + offset

    def order(t):
        p = jnp.where((t == 1) | (t == 4) | (t == 5) | (t == 7), 1, 0)
        q = jnp.where(t < 2, 0, jnp.where((t == 2) | (t == 4), 1, jnp.where(t < 6, 2, 3)))
        return p, q

    def keys_of(p, q):
        rel = jnp.where(q == 0, 2, jnp.where(q == 1, 1, jnp.where(q == 2, 3, 0)))
        return (((z_lo + p) % 2) * 4 + (y + rel) % 4) * 512

    def table(p, q, half):
        first = keys_of(p, q)
        k0 = half * (ROWS // 2)

        def one(k, size, m0=0, m=512, n0=0, n=512):
            keys = lax.broadcasted_iota(jnp.int32, (m, size), 0) + m0
            hot = (keys == (flipped[:, k : k + size] - first)).astype(F32).astype(BF16)
            return jnp.dot(hot, hl[k : k + size, n0 : n0 + n], preferred_element_type=F32)

        a, b = one(k0, 2048, 0, 256), one(k0, 2048, 256, 256)
        return jnp.concatenate([a[:, 0:256] + a[:, 256:512], b[:, 0:256] + b[:, 256:512]], axis=0)

    def first_half(t, p, q):
        v = table(p, q, 0)
        own[t, 0], own[t, 1] = v[0:256, 0:128], v[0:256, 128:256]
        part[t, 0], part[t, 1] = v[256:512, 0:128], v[256:512, 128:256]

    def second_half(t, p, q):
        v = table(p, q, 1)
        own[t, 0] = own[t, 0] + v[0:256, 0:128]
        own[t, 1] = own[t, 1] + v[0:256, 128:256]
        part[t, 0] = part[t, 0] + v[256:512, 0:128]
        part[t, 1] = part[t, 1] + v[256:512, 128:256]

    def swap(t):
        rc(part.at[t], land.at[t], d_s, d_r.at[t], partner).start()

    def ring_x_a(buf, la, s, r):
        far = ((x + 2) % 4) * 64
        rc(buf.at[rows(far, 32), :], la.at[0], s, r.at[0], xp).start()
        rc(buf.at[rows(far + 32, 32), :], la.at[1], s, r.at[1], xm).start()

    def ring_x_b(buf, la, lb, sa, ra, sb, rb):
        nxt, prv = ((x + 1) % 4) * 64, ((x + 3) % 4) * 64
        arrived(la.at[0], sa, ra.at[0])
        s = rows(nxt, 32)
        buf[s, :] = buf[s, :] + la[0]
        rc(buf.at[rows(nxt, 64), :], lb.at[0], sb, rb.at[0], xp).start()
        arrived(la.at[1], sa, ra.at[1])
        s = rows(prv + 32, 32)
        buf[s, :] = buf[s, :] + la[1]
        rc(buf.at[rows(prv, 64), :], lb.at[1], sb, rb.at[1], xm).start()

    def ring_x_c(buf, lb, sb, rb):
        arrived(lb.at[0], sb, rb.at[0])
        arrived(lb.at[1], sb, rb.at[1])
        return buf[rows(x * 64, 64), :] + lb[0] + lb[1]

    def ring_y(buf, half, q, la, lb, sa, ra, sb, rb, done):
        lo, hi = pl.ds(0, half), pl.ds(half, half)

        def far():
            rc(buf.at[lo, :], la.at[0], sa, ra.at[0], yp).start()
            rc(buf.at[hi, :], la.at[1], sa, ra.at[1], ym).start()

        def nxt():
            arrived(la.at[0], sa, ra.at[0])
            buf[lo, :] = buf[lo, :] + la[0]
            rc(buf, lb.at[0], sb, rb.at[0], yp).start()

        def prv():
            arrived(la.at[1], sa, ra.at[1])
            buf[hi, :] = buf[hi, :] + la[1]
            rc(buf, lb.at[1], sb, rb.at[1], ym).start()

        def home():
            arrived(lb.at[0], sb, rb.at[0])
            arrived(lb.at[1], sb, rb.at[1])
            done(buf[...] + lb[0] + lb[1])

        for k, fn in enumerate((far, nxt, prv, home)):
            when(q == k, fn)

    def stage1(t, p, q):
        arrived(land.at[t], d_s, d_r.at[t])
        own[t, 0] = own[t, 0] + land[t, 0]
        ring_x_a(own.at[t, 0], xa.at[t], xa_s, xa_r.at[t])
        own[t, 1] = own[t, 1] + land[t, 1]

        def done(v):
            yr[p] = v
            ring_x_a(yr.at[p], yxa.at[p], yxa_s, yxa_r.at[p])

        ring_y(
            own.at[t, 1], 128, q, ya.at[p], yb.at[p], ya_s, ya_r.at[p], yb_s, yb_r.at[p], done
        )

    def stage2(t, p, q):
        ring_x_b(own.at[t, 0], xa.at[t], xb.at[t], xa_s, xa_r.at[t], xb_s, xb_r.at[t])

        def tail():
            ring_x_b(yr.at[p], yxa.at[p], yxb.at[p], yxa_s, yxa_r.at[p], yxb_s, yxb_r.at[p])

        when(q == 3, tail)

    my_z = z_hi * 2 + z_lo

    def stage3(t, p, q):
        xr[t] = ring_x_c(own.at[t, 0], xb.at[t], xb_s, xb_r.at[t])

        def done(v):
            fin[p, 0] = v
            fin[p, 1] = ring_x_c(yr.at[p], yxb.at[p], yxb_s, yxb_r.at[p])
            zl = (z_lo + p) % 2
            for k in range(4):
                zh = (z_hi + k) % 4

                def send(zh=zh, k=k):
                    rc(
                        fin.at[p, :, rows(zh * 16, 16), :], zl_buf.at[my_z], z_s,
                        z_r.at[my_z], at(zl=zl, zh=zh),
                    ).start()

                when((p == 1) if k == 0 else True, send)

        ring_y(
            xr.at[t], 32, q, xya.at[p], xyb.at[p], xya_s, xya_r.at[p], xyb_s, xyb_r.at[p], done
        )

    first_half(0, 0, 0)
    second_half(0, 0, 0)
    pl.semaphore_wait(barrier, len(peers))
    swap(0)
    count_x()

    def late(stage, t):
        def go():
            stage(t, *order(t))

        when(t >= 0, go)

    def step(t, c):
        late(stage2, t - 3)
        when(t == 3, count_y)
        when(t == 5, count_z)
        first_half(t, *order(t))
        late(stage3, t - 4)
        late(stage1, t - 1)
        second_half(t, *order(t))
        swap(t)
        return c

    lax.fori_loop(1, UNITS, step, 0)

    stage2(5, 1, 2)
    stage3(4, 1, 1)
    stage1(7, 1, 3)
    stage2(6, 0, 3)
    stage3(5, 1, 2)

    total = cnt_y[...]
    for k in range(7):
        arrived(cz.at[k], cz_s, cz_r.at[k])
        total = total + cz[k]
    row = jnp.sum(
        jnp.where(lax.broadcasted_iota(jnp.int32, (8, 256), 0) == dom // 2, total, 0.0), axis=0, keepdims=True
    )
    mine = lax.broadcasted_iota(jnp.int32, (16, 256), 1) == (
        lax.broadcasted_iota(jnp.int32, (16, 256), 0) + rep * 16
    )
    column = jnp.sum(jnp.where(mine, row, 0.0), axis=1, keepdims=True)
    out_ref[:, 256:384] = jnp.broadcast_to(column, (16, 128))

    stage2(7, 1, 3)
    stage3(6, 0, 3)
    stage3(7, 1, 3)

    mine_rows = rows(z_hi * 16, 16)
    left, right = fin[0, 0, mine_rows, :], fin[0, 1, mine_rows, :]
    for k in range(1, 8):
        zh, zl = z_peer(k)
        z = zh * 2 + zl
        arrived(zl_buf.at[z], z_s, z_r.at[z])
        left = left + zl_buf[z, 0]
        right = right + zl_buf[z, 1]
    out_ref[:, 0:128] = left
    out_ref[:, 128:256] = right

    for buf, sem in (
        (part, d_s), (xa, xa_s), (xb, xb_s), (ya, ya_s), (yb, yb_s), (yxa, yxa_s), (yxb, yxb_s),
        (xya, xya_s), (xyb, xyb_s), (zl_buf.at[pl.ds(0, 7)], z_s), (cx, cx_s), (cy, cy_s), (cz, cz_s),
    ):
        sent(buf, sem)


def per_device(facts, row_owner, key_offset):
    dma = pltpu.SemaphoreType.DMA
    vm = pltpu.VMEM
    out = pl.pallas_call(
        kernel,
        out_shape=pltpu.VMEM((16, M + 128), F32),
        in_specs=[pl.BlockSpec(memory_space=pl.ANY)] * 3,
        out_specs=pl.BlockSpec(memory_space=vm),
        scratch_shapes=[
            vm((1, ROWS), jnp.int32), vm((1, ROWS), jnp.int32), vm((ROWS, M), F32), vm((ROWS, 2 * M), BF16),
            vm((8, 2, 256, 128), F32), vm((8, 2, 256, 128), F32), vm((8, 2, 256, 128), F32),
            vm((8, 2, 32, 128), F32), vm((8, 2, 64, 128), F32),
            vm((2, 2, 128, 128), F32), vm((2, 2, 256, 128), F32), vm((2, 256, 128), F32),
            vm((2, 2, 32, 128), F32), vm((2, 2, 64, 128), F32), vm((8, 64, 128), F32),
            vm((2, 2, 32, 128), F32), vm((2, 2, 64, 128), F32), vm((2, 2, 64, 128), F32),
            vm((8, 2, 16, 128), F32),
            vm((2, 8, 256), F32), vm((8, 256), F32), vm((8, 256), F32),
            vm((7, 8, 256), F32), vm((3, 8, 256), F32), vm((7, 8, 256), F32),
            dma((2,)), dma((8,)), dma, dma((8,)),
            dma, dma((8, 2)), dma, dma((8, 2)), dma, dma((2, 2)), dma, dma((2, 2)),
            dma, dma((2, 2)), dma, dma((2, 2)), dma, dma((2, 2)), dma, dma((2, 2)),
            dma, dma((8,)), dma, dma((7,)), dma, dma((3,)), dma, dma((7,)),
        ],
        compiler_params=pltpu.CompilerParams(
            collective_id=0, has_side_effects=True, vmem_limit_bytes=56 * 1024 * 1024
        ),
    )(row_owner.reshape(1, ROWS), key_offset.reshape(1, ROWS), facts)
    counts = out[:, M]
    return out[:, :M] / jnp.maximum(counts, 1.0)[:, None], counts


def solution(mesh):
    placed = (P(("dom", "rep"), None), P(("dom", "rep"), None), P(("dom", "rep")))
    return jax.shard_map(
        per_device,
        mesh=mesh,
        in_specs=placed,
        out_specs=(P(("dom", "rep"), None), P(("dom", "rep"))),
        check_vma=False,
    )
```

time: 61.3 us -> 45.6 us (0.74)
  Pallas kernels: 55.2 us -> 43.2 us
  local copies, waits for them, and re-layouts: 2.46 us -> 0 us
  other arithmetic: 2.06 us -> 1.31 us
    pallas_call x1, Pallas kernels: 55.2 us -> 43.2 us  [per_device(): pl.pallas_call(kernel, out_shape=pltpu.VMEM((16, M + 128), F32), in_specs...]
    unnamed x2 -> x0, local copies, waits for them, and re-layouts: 2.46 us -> none
    add x1 -> x0, other arithmetic: 1.33 us -> none  [per_device(): ids = (row_owner[:, 0] * 256 + key_offset).reshape(1, ROWS)]
    mul x1 -> x0, other arithmetic: 0.73 us -> none  [per_device(): ids = (row_owner[:, 0] * 256 + key_offset).reshape(1, ROWS)]
    div x0 -> x1, other arithmetic: none -> 0.68 us  [per_device(): return (out[:, :M] / jnp.maximum(counts, 1.0)[:, None], counts)]
    slice x0 -> x1, other arithmetic: none -> 0.63 us  [per_device(): counts = out[:, M]]
where the time goes in v2:
time: 45.6 us; the launch traced here: 45.1 us
  Pallas kernels  43.2 us (95%)
  other arithmetic  1.31 us (3%)
  between operations  0.64 us (1%)
    pallas_call x1, Pallas kernels, per_device(): pl.pallas_call(kernel, out_shape=pltpu.VMEM((16, M + 128), F32), in_specs...  43.2 us

profile of v2, /device:TPU:2, one launch (start us, length us, event | category | flops | bytes accessed | tf_op | source)
XLA Modules:
  0.0 45.1 jit_solution(627055203398233603)
XLA Ops:
  0.6 43.2 %shard_map.50 = f32[16,384]{1,0:T(8,128)S(1)} custom-call(s32[1,4096]{1,0:T(1,128)} %bitcast.2, s32[1,4096]{1,0:T(1,128)} %bitcast.3, f32[4096,256]{1,0:T(8,128)} %facts_ref.1), custom_call_target="tpu_custom_call" | custom-call | tf_op jit(solution)/shard_map/pallas_call | solution.py:330
  43.8 0.6 %slice_reduce_fusion = (f32[16]{0:T(128)}, f32[16]{0:T(128)S(1)}) fusion(f32[16,384]{1,0:T(8,128)S(1)} %shard_map.50), kind=kLoop, calls=%fused_computation.2 | loop fusion | flops 16 | bytes 192 | tf_op jit(solution)/shard_map/slice | solution.py:354
  44.4 0.7 %slice_divide_fusion = f32[16,256]{1,0:T(8,128)} fusion(f32[16,384]{1,0:T(8,128)S(1)} %shard_map.50, f32[16]{0:T(128)S(1)} %get-tuple-element.3), kind=kLoop, calls=%fused_computation | loop fusion | flops 4096 | bytes 32832 | tf_op jit(solution)/shard_map/div | solution.py:355

commit v3 on v2

v3 whole, which is shorter than its diff:
```python
import jax
import jax.numpy as jnp
from jax import lax
from jax.experimental import pallas as pl
from jax.experimental.pallas import tpu as pltpu
from jax.sharding import PartitionSpec as P

MESH = pl.DeviceIdType.MESH
ROWS = 4096
KEYS = 4096
M = 256
UNITS = 8
GROUPS = (
    ((2, 2), (1, 2), (2, 1), (3, 2)),
    ((2, 3), (0, 2), (2, 0), (1, 1)),
    ((1, 3), (3, 1), (3, 3), (0, 3)),
    ((0, 0), (0, 1), (1, 0), (3, 0)),
)
PLACE = {c: (g, i) for g, group in enumerate(GROUPS) for i, c in enumerate(group)}
F32 = jnp.float32
BF16 = jnp.bfloat16


def rows(start, size):
    return pl.ds(pl.multiple_of(start, size), size)


def kernel(
    owner_ref, offset_ref, facts_ref, means_ref, counts_ref,
    ownbuf, offbuf, fbuf, hl, own, part, land, fa, fb, res, sa, sb, fin, zl_buf,
    cnt, cnt_x, cnt_y, cx, cy, cz,
    i_sem, f_sem, d_s, d_r, fa_s, fa_r, fb_s, fb_r, sa_s, sa_r, sb_s, sb_r,
    z_s, z_r, cx_s, cx_r, cy_s, cy_r, cz_s, cz_r,
):
    dom, rep = lax.axis_index("dom"), lax.axis_index("rep")
    z_lo, y, core = dom // 8, (dom // 2) % 4, dom % 2
    x, z_hi = rep // 4, rep % 4

    def at(zl=z_lo, yy=y, cc=core, xx=x, zh=z_hi):
        return {"dom": zl * 8 + yy * 2 + cc, "rep": xx * 4 + zh}

    partner = at(cc=1 - core)
    xp, xm = at(xx=(x + 1) % 4), at(xx=(x + 3) % 4)
    yp, ym = at(yy=(y + 1) % 4), at(yy=(y + 3) % 4)

    def z_peer(k):
        z = (z_hi * 2 + z_lo + k) % 8
        return z // 2, z % 2

    peers = [partner]
    for k in range(1, 4):
        peers += [at(xx=(x + k) % 4), at(cc=1 - core, xx=(x + k) % 4), at(yy=(y + k) % 4)]
    for k in range(1, 8):
        zh, zl = z_peer(k)
        peers.append(at(zl=zl, zh=zh))

    def rc(src, dst, ss, rs, dev):
        return pltpu.make_async_remote_copy(
            src_ref=src, dst_ref=dst, send_sem=ss, recv_sem=rs, device_id=dev, device_id_type=MESH
        )

    def arrived(buf, ss, rs):
        rc(buf, buf, ss, rs, partner).wait_recv()

    def sent(buf, ss):
        rc(buf, buf, ss, d_r.at[0], partner).wait_send()

    def f_copy(i):
        s = pl.ds(i * 512, 512)
        return pltpu.make_async_copy(facts_ref.at[s, :], fbuf.at[s, :], f_sem.at[i])

    i_copies = (
        pltpu.make_async_copy(owner_ref, ownbuf, i_sem.at[0]),
        pltpu.make_async_copy(offset_ref, offbuf, i_sem.at[1]),
    )
    for c in i_copies:
        c.start()
    barrier = pltpu.get_barrier_semaphore()
    for p in peers:
        pl.semaphore_signal(barrier, inc=1, device_id=p, device_id_type=MESH)

    for i in range(8):
        f_copy(i).start()
    for c in i_copies:
        c.wait()

    owner, offset = ownbuf[...], offbuf[...]
    high = (owner % 2) * 16 + (owner // 2) * 2 + offset // 128
    high_hot = (lax.broadcasted_iota(jnp.int32, (32, ROWS), 0) == high).astype(F32).astype(BF16)
    low_hot = (lax.broadcasted_iota(jnp.int32, (128, ROWS), 0) == offset % 128).astype(F32).astype(BF16)
    counts = lax.dot_general(high_hot, low_hot, (((1,), (1,)), ((), ())), preferred_element_type=F32)
    cnt[0], cnt[1] = counts[0:16], counts[16:32]

    def count_x():
        for k in range(1, 8):
            cc, xx = (core + k // 4) % 2, (x + k) % 4
            rc(cnt.at[cc], cx.at[k - 1], cx_s, cx_r.at[k - 1], at(cc=cc, xx=xx)).start()

    def count_y():
        total = cnt[core]
        for k in range(7):
            arrived(cx.at[k], cx_s, cx_r.at[k])
            total = total + cx[k]
        cnt_x[...] = total
        for k in range(1, 4):
            rc(cnt_x, cy.at[k - 1], cy_s, cy_r.at[k - 1], at(yy=(y + k) % 4)).start()

    def count_z():
        total = cnt_x[...]
        for k in range(3):
            arrived(cy.at[k], cy_s, cy_r.at[k])
            total = total + cy[k]
        cnt_y[...] = total
        for k in range(1, 8):
            zh, zl = z_peer(k)
            rc(cnt_y, cz.at[k - 1], cz_s, cz_r.at[k - 1], at(zl=zl, zh=zh)).start()

    for i in range(8):
        f_copy(i).wait()

        def split(j, c, i=i):
            s = rows(i * 512 + j * 128, 128)
            v = fbuf[s, :]
            h = v.astype(BF16)
            hl[s, 0:256] = h
            hl[s, 256:512] = (v - h.astype(F32)).astype(BF16)
            return c

        lax.fori_loop(0, 4, split, 0)

    ids = owner * 256 + offset

    def table(t, half, of):
        g, p = t // 2, t % 2
        k = half * (ROWS // 2)
        part_ids = ids[:, k : k + ROWS // 2]
        keys = lax.broadcasted_iota(jnp.int32, (64, ROWS // 2), 0)
        hot = []
        for dx, dy in GROUPS[g]:
            dest = at(zl=(z_lo + p) % 2, yy=(y + dy) % 4, cc=of, xx=(x + dx) % 4, zh=0)
            hot.append((keys == part_ids - (dest["dom"] * 256 + dest["rep"] * 16)).astype(F32).astype(BF16))
        acc = jnp.dot(jnp.concatenate(hot, axis=0), hl[k : k + ROWS // 2, :], preferred_element_type=F32)
        return acc[:, 0:256] + acc[:, 256:512]

    def first_half(t):
        v, w = table(t, 0, core), table(t, 0, 1 - core)
        own[t, 0], own[t, 1] = v[:, 0:128], v[:, 128:256]
        part[t, 0], part[t, 1] = w[:, 0:128], w[:, 128:256]

    def second_half(t):
        v, w = table(t, 1, core), table(t, 1, 1 - core)
        own[t, 0] = own[t, 0] + v[:, 0:128]
        own[t, 1] = own[t, 1] + v[:, 128:256]
        part[t, 0] = part[t, 0] + w[:, 0:128]
        part[t, 1] = part[t, 1] + w[:, 128:256]

    def swap(t):
        rc(part.at[t], land.at[t], d_s, d_r.at[t], partner).start()

    along = ((xp, xm), (yp, ym))

    def block(k, p, d, e, start=0, size=64):
        g, i = PLACE[(d, e) if k == 0 else (e, d)]
        return own.at[2 * g + p, k, pl.ds(i * 64 + start, size), :]

    def add_in(buf, start, landed, ss, rs):
        arrived(landed, ss, rs)
        r = pl.ds(start, 32)
        buf[r, :] = buf[r, :] + landed[...]

    def far(k, p, e):
        for w in range(2):
            rc(block(k, p, 2, e, 32 * w, 32), fa.at[p, k, e, w], fa_s, fa_r.at[p, k, e, w], along[k][w]).start()

    def near(k, p, e, w):
        buf = block(k, p, 1 + 2 * w, e)
        add_in(buf, 32 * w, fa.at[p, k, e, w], fa_s, fa_r.at[p, k, e, w])
        rc(buf, fb.at[p, k, e, w], fb_s, fb_r.at[p, k, e, w], along[k][w]).start()

    def home(k, p, e):
        for w in range(2):
            arrived(fb.at[p, k, e, w], fb_s, fb_r.at[p, k, e, w])
        res[p, k, e] = block(k, p, 0, e)[...] + fb[p, k, e, 0] + fb[p, k, e, 1]

    def far2(k, p):
        for w in range(2):
            rc(res.at[p, k, 2, pl.ds(32 * w, 32), :], sa.at[p, k, w], sa_s, sa_r.at[p, k, w], along[1 - k][w]).start()

    def near2(k, p, w):
        buf = res.at[p, k, 1 + 2 * w]
        add_in(buf, 32 * w, sa.at[p, k, w], sa_s, sa_r.at[p, k, w])
        rc(buf, sb.at[p, k, w], sb_s, sb_r.at[p, k, w], along[1 - k][w]).start()

    def home2(k, p):
        for w in range(2):
            arrived(sb.at[p, k, w], sb_s, sb_r.at[p, k, w])
        fin[p, k] = res[p, k, 0] + sb[p, k, 0] + sb[p, k, 1]

    def join(t):
        arrived(land.at[t], d_s, d_r.at[t])
        own[t, 0] = own[t, 0] + land[t, 0]
        own[t, 1] = own[t, 1] + land[t, 1]

    def stage0(p):
        join(p)
        far(0, p, 2)
        far(1, p, 2)
        far(0, p, 1)
        far(1, p, 1)
        far(1, p, 3)

    def stage0b(p):
        near(0, p, 2, 0)
        near(0, p, 2, 1)
        near(1, p, 2, 0)

    def stage1(p):
        join(2 + p)
        far(0, p, 3)
        far(0, p, 0)
        far(1, p, 0)
        near(1, p, 2, 1)
        near(0, p, 1, 0)
        near(1, p, 1, 0)

    def stage2(p):
        join(4 + p)
        home(0, p, 2)
        far2(0, p)
        home(1, p, 2)
        far2(1, p)
        near(0, p, 1, 1)
        near(1, p, 1, 1)
        near(0, p, 3, 0)
        near(1, p, 3, 0)
        near(0, p, 3, 1)
        near(1, p, 3, 1)
        near(1, p, 0, 1)

    def stage2b(p):
        home(0, p, 3)
        near2(0, p, 1)

    def stage3(p):
        join(6 + p)
        near(0, p, 0, 0)
        near(0, p, 0, 1)
        near(1, p, 0, 0)
        home(1, p, 1)
        near2(1, p, 0)
        home(1, p, 3)
        near2(1, p, 1)
        home(0, p, 1)
        near2(0, p, 0)

    my_z = z_hi * 2 + z_lo

    def last(p):
        for k in range(2):
            home(k, p, 0)
            home2(k, p)
        for k in range(1 - p, 4):
            zh = (z_hi + k) % 4
            rc(
                fin.at[p, :, rows(zh * 16, 16), :], zl_buf.at[my_z], z_s, z_r.at[my_z],
                at(zl=(z_lo + p) % 2, zh=zh),
            ).start()

    stages = (stage0, stage1, stage2, stage3)
    early = {3: (stage0b, 0), 4: (stage0b, 1), 7: (stage2b, 0)}
    for t in range(UNITS):
        if t in early:
            early[t][0](early[t][1])
        if t == 3:
            count_y()
        if t == 5:
            count_z()
        first_half(t)
        if t:
            stages[(t - 1) // 2]((t - 1) % 2)
        second_half(t)
        if t == 0:
            pl.semaphore_wait(barrier, len(peers))
        swap(t)
        if t == 0:
            count_x()

    stage2b(1)
    stage3(1)

    total = cnt_y[...]
    for k in range(7):
        arrived(cz.at[k], cz_s, cz_r.at[k])
        total = total + cz[k]
    row = jnp.sum(
        jnp.where(lax.broadcasted_iota(jnp.int32, (16, 128), 0) == (dom // 2) * 2 + x // 2, total, 0.0),
        axis=0, keepdims=True,
    )
    mine = lax.broadcasted_iota(jnp.int32, (16, 128), 1) == (
        lax.broadcasted_iota(jnp.int32, (16, 128), 0) + (x % 2) * 64 + z_hi * 16
    )
    column = jnp.sum(jnp.where(mine, row, 0.0), axis=1, keepdims=True)
    eye = lax.broadcasted_iota(jnp.int32, (16, 16), 0) == lax.broadcasted_iota(jnp.int32, (16, 16), 1)
    counts_ref[...] = jnp.sum(jnp.where(eye, column, 0.0), axis=0, keepdims=True)
    divisor = jnp.maximum(column, 1.0)

    last(0)
    last(1)

    mine_rows = rows(z_hi * 16, 16)
    left, right = fin[0, 0, mine_rows, :], fin[0, 1, mine_rows, :]
    for k in range(1, 8):
        zh, zl = z_peer(k)
        z = zh * 2 + zl
        arrived(zl_buf.at[z], z_s, z_r.at[z])
        left = left + zl_buf[z, 0]
        right = right + zl_buf[z, 1]
    means_ref[:, 0:128] = left / divisor
    means_ref[:, 128:256] = right / divisor

    for buf, sem in (
        (part, d_s), (fa, fa_s), (fb, fb_s), (sa, sa_s), (sb, sb_s),
        (zl_buf.at[pl.ds(0, 7)], z_s), (cx, cx_s), (cy, cy_s), (cz, cz_s),
    ):
        sent(buf, sem)


def per_device(facts, row_owner, key_offset):
    dma = pltpu.SemaphoreType.DMA
    vm = pltpu.VMEM
    means, counts = pl.pallas_call(
        kernel,
        out_shape=(pltpu.VMEM((16, M), F32), pltpu.VMEM((1, 16), F32)),
        in_specs=[pl.BlockSpec(memory_space=pl.ANY)] * 3,
        out_specs=(pl.BlockSpec(memory_space=vm), pl.BlockSpec(memory_space=vm)),
        scratch_shapes=[
            vm((1, ROWS), jnp.int32), vm((1, ROWS), jnp.int32), vm((ROWS, M), F32), vm((ROWS, 2 * M), BF16),
            vm((8, 2, 256, 128), F32), vm((8, 2, 256, 128), F32), vm((8, 2, 256, 128), F32),
            vm((2, 2, 4, 2, 32, 128), F32), vm((2, 2, 4, 2, 64, 128), F32), vm((2, 2, 4, 64, 128), F32),
            vm((2, 2, 2, 32, 128), F32), vm((2, 2, 2, 64, 128), F32), vm((2, 2, 64, 128), F32),
            vm((8, 2, 16, 128), F32),
            vm((2, 16, 128), F32), vm((16, 128), F32), vm((16, 128), F32),
            vm((7, 16, 128), F32), vm((3, 16, 128), F32), vm((7, 16, 128), F32),
            dma((2,)), dma((8,)), dma, dma((8,)),
            dma, dma((2, 2, 4, 2)), dma, dma((2, 2, 4, 2)), dma, dma((2, 2, 2)), dma, dma((2, 2, 2)),
            dma, dma((8,)), dma, dma((7,)), dma, dma((3,)), dma, dma((7,)),
        ],
        compiler_params=pltpu.CompilerParams(
            collective_id=0, has_side_effects=True, vmem_limit_bytes=56 * 1024 * 1024
        ),
    )(row_owner.reshape(1, ROWS), key_offset.reshape(1, ROWS), facts)
    return means, counts.reshape(16)


def solution(mesh):
    placed = (P(("dom", "rep"), None), P(("dom", "rep"), None), P(("dom", "rep")))
    return jax.shard_map(
        per_device,
        mesh=mesh,
        in_specs=placed,
        out_specs=(P(("dom", "rep"), None), P(("dom", "rep"))),
        check_vma=False,
    )
```

time: 45.6 us -> 43.9 us (0.963)
  Pallas kernels: 43.2 us -> 41.4 us
  other arithmetic: 1.31 us -> 0 us
  local copies, waits for them, and re-layouts: 0 us -> 1.12 us
    pallas_call x1, Pallas kernels: 43.2 us -> 41.4 us  [per_device(): pl.pallas_call(kernel, out_shape=(pltpu.VMEM((16, M), F32), pltpu.VMEM((1...]
    unnamed x0 -> x2, local copies, waits for them, and re-layouts: none -> 1.12 us
    div x1 -> x0, other arithmetic: 0.68 us -> none  [per_device(): return (out[:, :M] / jnp.maximum(counts, 1.0)[:, None], counts)]
    slice x1 -> x0, other arithmetic: 0.63 us -> none  [per_device(): counts = out[:, M]]
where the time goes in v3:
time: 43.9 us; the launch traced here: 43.1 us
  Pallas kernels  41.4 us (94%)
  local copies, waits for them, and re-layouts  1.12 us (3%)
  between operations  0.64 us (1%)
    pallas_call x1, Pallas kernels, per_device(): pl.pallas_call(kernel, out_shape=(pltpu.VMEM((16, M), F32), pltpu.VMEM((1...  41.4 us
    unnamed x2, local copies, waits for them, and re-layouts  1.12 us

profile of v3, /device:TPU:2, one launch (start us, length us, event | category | flops | bytes accessed | tf_op | source)
XLA Modules:
  0.0 43.1 jit_solution(4102406503462743528)
XLA Ops:
  0.6 41.4 %shard_map.50 = (f32[16,256]{1,0:T(8,128)S(1)}, f32[1,16]{1,0:T(1,128)S(1)}) custom-call(s32[1,4096]{1,0:T(1,128)} %bitcast.4, s32[1,4096]{1,0:T(1,128)} %bitcast.5, f32[4096,256]{1,0:T(8,128)} %facts_ref.1), custom_call_target="tpu_custom_call" | custom-call | tf_op jit(solution)/shard_map/pallas_call | solution.py:331
  42.0 0.6 %copy.7 = f32[16,256]{1,0:T(8,128)} copy(f32[16,256]{1,0:T(8,128)S(1)} %get-tuple-element.6) | data formatting | bytes 32768
  42.6 0.5 %copy.8 = f32[16]{0:T(128)} copy(f32[16]{0:T(128)S(1)} %bitcast.3) | data formatting | bytes 128

commit v4 on v3

--- a/solution.py
+++ b/solution.py
@@ -19,6 +19,7 @@
 PLACE = {c: (g, i) for g, group in enumerate(GROUPS) for i, c in enumerate(group)}
 F32 = jnp.float32
 BF16 = jnp.bfloat16
+F8 = jnp.float8_e4m3fn
 
 
 def rows(start, size):
@@ -115,18 +116,29 @@
             zh, zl = z_peer(k)
             rc(cnt_y, cz.at[k - 1], cz_s, cz_r.at[k - 1], at(zl=zl, zh=zh)).start()
 
+    top = jnp.zeros((8, 256), F32)
     for i in range(8):
         f_copy(i).wait()
 
-        def split(j, c, i=i):
-            s = rows(i * 512 + j * 128, 128)
-            v = fbuf[s, :]
-            h = v.astype(BF16)
-            hl[s, 0:256] = h
-            hl[s, 256:512] = (v - h.astype(F32)).astype(BF16)
-            return c
-
-        lax.fori_loop(0, 4, split, 0)
+        def peak(j, c, i=i):
+            v = jnp.abs(fbuf[rows(i * 512 + j * 256, 256), :])
+            return jnp.maximum(c, jnp.max(v.reshape(32, 8, 256), axis=0))
+
+        top = lax.fori_loop(0, 2, peak, top)
+    top = jnp.max(jnp.max(top, axis=0, keepdims=True), axis=1, keepdims=True)
+    scale = jnp.minimum(256.0 / top, 2.0**126)
+    unscale = 1.0 / scale
+
+    def split(j, c):
+        s = rows(j * 128, 128)
+        v = fbuf[s, :] * scale
+        for k in range(3):
+            h = v.astype(F8)
+            hl[s, k * 256 : (k + 1) * 256] = h
+            v = (v - h.astype(F32)) * 16.0
+        return c
+
+    lax.fori_loop(0, ROWS // 128, split, 0)
 
     ids = owner * 256 + offset
 
@@ -138,9 +150,9 @@
         hot = []
         for dx, dy in GROUPS[g]:
             dest = at(zl=(z_lo + p) % 2, yy=(y + dy) % 4, cc=of, xx=(x + dx) % 4, zh=0)
-            hot.append((keys == part_ids - (dest["dom"] * 256 + dest["rep"] * 16)).astype(F32).astype(BF16))
+            hot.append((keys == part_ids - (dest["dom"] * 256 + dest["rep"] * 16)).astype(F32).astype(F8))
         acc = jnp.dot(jnp.concatenate(hot, axis=0), hl[k : k + ROWS // 2, :], preferred_element_type=F32)
-        return acc[:, 0:256] + acc[:, 256:512]
+        return (acc[:, 0:256] + acc[:, 256:512] * (1 / 16) + acc[:, 512:768] * (1 / 256)) * unscale
 
     def first_half(t):
         v, w = table(t, 0, core), table(t, 0, 1 - core)
@@ -267,23 +279,33 @@
             ).start()
 
     stages = (stage0, stage1, stage2, stage3)
-    early = {3: (stage0b, 0), 4: (stage0b, 1), 7: (stage2b, 0)}
-    for t in range(UNITS):
-        if t in early:
-            early[t][0](early[t][1])
+    def before(t):
+        if t >= 2:
+            if t in (4, 5):
+                stage0b(t - 4)
+            stages[(t - 2) // 2](t % 2)
         if t == 3:
             count_y()
         if t == 5:
             count_z()
+
+    for t in range(UNITS - 1):
+        before(t)
         first_half(t)
-        if t:
-            stages[(t - 1) // 2]((t - 1) % 2)
         second_half(t)
         if t == 0:
             pl.semaphore_wait(barrier, len(peers))
         swap(t)
         if t == 0:
             count_x()
+    before(7)
+    w0, w1 = table(7, 0, 1 - core), table(7, 1, 1 - core)
+    part[7, 0], part[7, 1] = w0[:, 0:128] + w1[:, 0:128], w0[:, 128:256] + w1[:, 128:256]
+    swap(7)
+    stage2b(0)
+    stage3(0)
+    v0, v1 = table(7, 0, core), table(7, 1, core)
+    own[7, 0], own[7, 1] = v0[:, 0:128] + v1[:, 0:128], v0[:, 128:256] + v1[:, 128:256]
 
     stage2b(1)
     stage3(1)
@@ -334,7 +356,7 @@
         in_specs=[pl.BlockSpec(memory_space=pl.ANY)] * 3,
         out_specs=(pl.BlockSpec(memory_space=vm), pl.BlockSpec(memory_space=vm)),
         scratch_shapes=[
-            vm((1, ROWS), jnp.int32), vm((1, ROWS), jnp.int32), vm((ROWS, M), F32), vm((ROWS, 2 * M), BF16),
+            vm((1, ROWS), jnp.int32), vm((1, ROWS), jnp.int32), vm((ROWS, M), F32), vm((ROWS, 3 * M), F8),
             vm((8, 2, 256, 128), F32), vm((8, 2, 256, 128), F32), vm((8, 2, 256, 128), F32),
             vm((2, 2, 4, 2, 32, 128), F32), vm((2, 2, 4, 2, 64, 128), F32), vm((2, 2, 4, 64, 128), F32),
             vm((2, 2, 2, 32, 128), F32), vm((2, 2, 2, 64, 128), F32), vm((2, 2, 64, 128), F32),

time: 43.9 us -> 39.8 us (0.907); the launches traced: 43.1 us -> 39.7 us
  Pallas kernels: 41.4 us -> 37.9 us
    pallas_call x1, Pallas kernels: 41.4 us -> 37.9 us  [per_device(): pl.pallas_call(kernel, out_shape=(pltpu.VMEM((16, M), F32), pltpu.VMEM((1...]
where the time goes in v4:
time: 39.8 us; the launch traced here: 39.7 us
  Pallas kernels  37.9 us (95%)
  local copies, waits for them, and re-layouts  1.12 us (3%)
  between operations  0.64 us (2%)
    pallas_call x1, Pallas kernels, per_device(): pl.pallas_call(kernel, out_shape=(pltpu.VMEM((16, M), F32), pltpu.VMEM((1...  37.9 us
    unnamed x2, local copies, waits for them, and re-layouts  1.12 us

profile of v4, /device:TPU:2, one launch (start us, length us, event | category | flops | bytes accessed | tf_op | source)
XLA Modules:
  0.0 39.7 jit_solution(11647784054819609776)
XLA Ops:
  0.6 37.9 %shard_map.50 = (f32[16,256]{1,0:T(8,128)S(1)}, f32[1,16]{1,0:T(1,128)S(1)}) custom-call(s32[1,4096]{1,0:T(1,128)} %bitcast.4, s32[1,4096]{1,0:T(1,128)} %bitcast.5, f32[4096,256]{1,0:T(8,128)} %facts_ref.1), custom_call_target="tpu_custom_call" | custom-call | tf_op jit(solution)/shard_map/pallas_call | solution.py:353
  38.6 0.6 %copy.7 = f32[16,256]{1,0:T(8,128)} copy(f32[16,256]{1,0:T(8,128)S(1)} %get-tuple-element.6) | data formatting | bytes 32768
  39.2 0.5 %copy.8 = f32[16]{0:T(128)} copy(f32[16]{0:T(128)S(1)} %bitcast.3) | data formatting | bytes 128

commit v5 on v4

--- a/solution.py
+++ b/solution.py
@@ -67,7 +67,7 @@
         rc(buf, buf, ss, d_r.at[0], partner).wait_send()
 
     def f_copy(i):
-        s = pl.ds(i * 512, 512)
+        s = pl.ds(i * 1024, 1024)
         return pltpu.make_async_copy(facts_ref.at[s, :], fbuf.at[s, :], f_sem.at[i])
 
     i_copies = (
@@ -80,7 +80,7 @@
     for p in peers:
         pl.semaphore_signal(barrier, inc=1, device_id=p, device_id_type=MESH)
 
-    for i in range(8):
+    for i in range(4):
         f_copy(i).start()
     for c in i_copies:
         c.wait()
@@ -95,36 +95,36 @@
     def count_x():
         for k in range(1, 8):
             cc, xx = (core + k // 4) % 2, (x + k) % 4
-            rc(cnt.at[cc], cx.at[k - 1], cx_s, cx_r.at[k - 1], at(cc=cc, xx=xx)).start()
+            rc(cnt.at[cc], cx.at[k - 1], cx_s, cx_r, at(cc=cc, xx=xx)).start()
 
     def count_y():
         total = cnt[core]
+        arrived(cx, cx_s, cx_r)
         for k in range(7):
-            arrived(cx.at[k], cx_s, cx_r.at[k])
             total = total + cx[k]
         cnt_x[...] = total
         for k in range(1, 4):
-            rc(cnt_x, cy.at[k - 1], cy_s, cy_r.at[k - 1], at(yy=(y + k) % 4)).start()
+            rc(cnt_x, cy.at[k - 1], cy_s, cy_r, at(yy=(y + k) % 4)).start()
 
     def count_z():
         total = cnt_x[...]
+        arrived(cy, cy_s, cy_r)
         for k in range(3):
-            arrived(cy.at[k], cy_s, cy_r.at[k])
             total = total + cy[k]
         cnt_y[...] = total
         for k in range(1, 8):
             zh, zl = z_peer(k)
-            rc(cnt_y, cz.at[k - 1], cz_s, cz_r.at[k - 1], at(zl=zl, zh=zh)).start()
+            rc(cnt_y, cz.at[k - 1], cz_s, cz_r, at(zl=zl, zh=zh)).start()
 
     top = jnp.zeros((8, 256), F32)
-    for i in range(8):
+    for i in range(4):
         f_copy(i).wait()
 
         def peak(j, c, i=i):
-            v = jnp.abs(fbuf[rows(i * 512 + j * 256, 256), :])
+            v = jnp.abs(fbuf[rows(i * 1024 + j * 256, 256), :])
             return jnp.maximum(c, jnp.max(v.reshape(32, 8, 256), axis=0))
 
-        top = lax.fori_loop(0, 2, peak, top)
+        top = lax.fori_loop(0, 4, peak, top)
     top = jnp.max(jnp.max(top, axis=0, keepdims=True), axis=1, keepdims=True)
     scale = jnp.minimum(256.0 / top, 2.0**126)
     unscale = 1.0 / scale
@@ -175,37 +175,43 @@
         g, i = PLACE[(d, e) if k == 0 else (e, d)]
         return own.at[2 * g + p, k, pl.ds(i * 64 + start, size), :]
 
-    def add_in(buf, start, landed, ss, rs):
-        arrived(landed, ss, rs)
+    waited = set()
+
+    def both(name, buf, ss, rs):
+        if name not in waited:
+            waited.add(name)
+            arrived(buf, ss, rs)
+
+    def add_in(buf, start, landed):
         r = pl.ds(start, 32)
         buf[r, :] = buf[r, :] + landed[...]
 
     def far(k, p, e):
         for w in range(2):
-            rc(block(k, p, 2, e, 32 * w, 32), fa.at[p, k, e, w], fa_s, fa_r.at[p, k, e, w], along[k][w]).start()
+            rc(block(k, p, 2, e, 32 * w, 32), fa.at[p, k, e, w], fa_s, fa_r.at[p, k, e], along[k][w]).start()
 
     def near(k, p, e, w):
         buf = block(k, p, 1 + 2 * w, e)
-        add_in(buf, 32 * w, fa.at[p, k, e, w], fa_s, fa_r.at[p, k, e, w])
-        rc(buf, fb.at[p, k, e, w], fb_s, fb_r.at[p, k, e, w], along[k][w]).start()
+        both((0, p, k, e), fa.at[p, k, e], fa_s, fa_r.at[p, k, e])
+        add_in(buf, 32 * w, fa.at[p, k, e, w])
+        rc(buf, fb.at[p, k, e, w], fb_s, fb_r.at[p, k, e], along[k][w]).start()
 
     def home(k, p, e):
-        for w in range(2):
-            arrived(fb.at[p, k, e, w], fb_s, fb_r.at[p, k, e, w])
+        arrived(fb.at[p, k, e], fb_s, fb_r.at[p, k, e])
         res[p, k, e] = block(k, p, 0, e)[...] + fb[p, k, e, 0] + fb[p, k, e, 1]
 
     def far2(k, p):
         for w in range(2):
-            rc(res.at[p, k, 2, pl.ds(32 * w, 32), :], sa.at[p, k, w], sa_s, sa_r.at[p, k, w], along[1 - k][w]).start()
+            rc(res.at[p, k, 2, pl.ds(32 * w, 32), :], sa.at[p, k, w], sa_s, sa_r.at[p, k], along[1 - k][w]).start()
 
     def near2(k, p, w):
         buf = res.at[p, k, 1 + 2 * w]
-        add_in(buf, 32 * w, sa.at[p, k, w], sa_s, sa_r.at[p, k, w])
-        rc(buf, sb.at[p, k, w], sb_s, sb_r.at[p, k, w], along[1 - k][w]).start()
+        both((1, p, k), sa.at[p, k], sa_s, sa_r.at[p, k])
+        add_in(buf, 32 * w, sa.at[p, k, w])
+        rc(buf, sb.at[p, k, w], sb_s, sb_r.at[p, k], along[1 - k][w]).start()
 
     def home2(k, p):
-        for w in range(2):
-            arrived(sb.at[p, k, w], sb_s, sb_r.at[p, k, w])
+        arrived(sb.at[p, k], sb_s, sb_r.at[p, k])
         fin[p, k] = res[p, k, 0] + sb[p, k, 0] + sb[p, k, 1]
 
     def join(t):
@@ -274,7 +280,7 @@
         for k in range(1 - p, 4):
             zh = (z_hi + k) % 4
             rc(
-                fin.at[p, :, rows(zh * 16, 16), :], zl_buf.at[my_z], z_s, z_r.at[my_z],
+                fin.at[p, :, rows(zh * 16, 16), :], zl_buf.at[my_z], z_s, z_r,
                 at(zl=(z_lo + p) % 2, zh=zh),
             ).start()
 
@@ -311,8 +317,8 @@
     stage3(1)
 
     total = cnt_y[...]
+    arrived(cz, cz_s, cz_r)
     for k in range(7):
-        arrived(cz.at[k], cz_s, cz_r.at[k])
         total = total + cz[k]
     row = jnp.sum(
         jnp.where(lax.broadcasted_iota(jnp.int32, (16, 128), 0) == (dom // 2) * 2 + x // 2, total, 0.0),
@@ -329,12 +335,12 @@
     last(0)
     last(1)
 
+    arrived(zl_buf.at[pl.ds(0, 7)], z_s, z_r)
     mine_rows = rows(z_hi * 16, 16)
     left, right = fin[0, 0, mine_rows, :], fin[0, 1, mine_rows, :]
     for k in range(1, 8):
         zh, zl = z_peer(k)
         z = zh * 2 + zl
-        arrived(zl_buf.at[z], z_s, z_r.at[z])
         left = left + zl_buf[z, 0]
         right = right + zl_buf[z, 1]
     means_ref[:, 0:128] = left / divisor
@@ -363,9 +369,9 @@
             vm((8, 2, 16, 128), F32),
             vm((2, 16, 128), F32), vm((16, 128), F32), vm((16, 128), F32),
             vm((7, 16, 128), F32), vm((3, 16, 128), F32), vm((7, 16, 128), F32),
-            dma((2,)), dma((8,)), dma, dma((8,)),
-            dma, dma((2, 2, 4, 2)), dma, dma((2, 2, 4, 2)), dma, dma((2, 2, 2)), dma, dma((2, 2, 2)),
-            dma, dma((8,)), dma, dma((7,)), dma, dma((3,)), dma, dma((7,)),
+            dma((2,)), dma((4,)), dma, dma((8,)),
+            dma, dma((2, 2, 4)), dma, dma((2, 2, 4)), dma, dma((2, 2)), dma, dma((2, 2)),
+            dma, dma, dma, dma, dma, dma, dma, dma,
         ],
         compiler_params=pltpu.CompilerParams(
             collective_id=0, has_side_effects=True, vmem_limit_bytes=56 * 1024 * 1024

time: 39.8 us -> 39.3 us (0.987)
  Pallas kernels: 37.9 us -> 37.4 us
    pallas_call x1, Pallas kernels: 37.9 us -> 37.4 us  [per_device(): pl.pallas_call(kernel, out_shape=(pltpu.VMEM((16, M), F32), pltpu.VMEM((1...]
where the time goes in v5:
time: 39.3 us; the launch traced here: 39.1 us
  Pallas kernels  37.4 us (95%)
  local copies, waits for them, and re-layouts  1.12 us (3%)
  between operations  0.64 us (2%)
    pallas_call x1, Pallas kernels, per_device(): pl.pallas_call(kernel, out_shape=(pltpu.VMEM((16, M), F32), pltpu.VMEM((1...  37.4 us
    unnamed x2, local copies, waits for them, and re-layouts  1.12 us

profile of v5, /device:TPU:2, one launch (start us, length us, event | category | flops | bytes accessed | tf_op | source)
XLA Modules:
  0.0 39.1 jit_solution(6683858174661128658)
XLA Ops:
  0.6 37.4 %shard_map.50 = (f32[16,256]{1,0:T(8,128)S(1)}, f32[1,16]{1,0:T(1,128)S(1)}) custom-call(s32[1,4096]{1,0:T(1,128)} %bitcast.4, s32[1,4096]{1,0:T(1,128)} %bitcast.5, f32[4096,256]{1,0:T(8,128)} %facts_ref.1), custom_call_target="tpu_custom_call" | custom-call | tf_op jit(solution)/shard_map/pallas_call | solution.py:359
  38.0 0.6 %copy.7 = f32[16,256]{1,0:T(8,128)} copy(f32[16,256]{1,0:T(8,128)S(1)} %get-tuple-element.6) | data formatting | bytes 32768
  38.6 0.5 %copy.8 = f32[16]{0:T(128)} copy(f32[16]{0:T(128)S(1)} %bitcast.3) | data formatting | bytes 128

commit v6 on v5

--- a/solution.py
+++ b/solution.py
@@ -17,6 +17,7 @@
     ((0, 0), (0, 1), (1, 0), (3, 0)),
 )
 PLACE = {c: (g, i) for g, group in enumerate(GROUPS) for i, c in enumerate(group)}
+FIRST = 1024
 F32 = jnp.float32
 BF16 = jnp.bfloat16
 F8 = jnp.float8_e4m3fn
@@ -129,29 +130,31 @@
     scale = jnp.minimum(256.0 / top, 2.0**126)
     unscale = 1.0 / scale
 
-    def split(j, c):
-        s = rows(j * 128, 128)
+    def split(s):
         v = fbuf[s, :] * scale
         for k in range(3):
             h = v.astype(F8)
             hl[s, k * 256 : (k + 1) * 256] = h
             v = (v - h.astype(F32)) * 16.0
+
+    def split_first(j, c):
+        split(rows(j * 128, 128))
         return c
 
-    lax.fori_loop(0, ROWS // 128, split, 0)
+    lax.fori_loop(0, FIRST // 128, split_first, 0)
 
     ids = owner * 256 + offset
 
-    def table(t, half, of):
+    def table(t, half, of, size=ROWS // 2):
         g, p = t // 2, t % 2
-        k = half * (ROWS // 2)
-        part_ids = ids[:, k : k + ROWS // 2]
-        keys = lax.broadcasted_iota(jnp.int32, (64, ROWS // 2), 0)
+        k = half * size
+        part_ids = ids[:, k : k + size]
+        keys = lax.broadcasted_iota(jnp.int32, (64, size), 0)
         hot = []
         for dx, dy in GROUPS[g]:
             dest = at(zl=(z_lo + p) % 2, yy=(y + dy) % 4, cc=of, xx=(x + dx) % 4, zh=0)
             hot.append((keys == part_ids - (dest["dom"] * 256 + dest["rep"] * 16)).astype(F32).astype(F8))
-        acc = jnp.dot(jnp.concatenate(hot, axis=0), hl[k : k + ROWS // 2, :], preferred_element_type=F32)
+        acc = jnp.dot(jnp.concatenate(hot, axis=0), hl[k : k + size, :], preferred_element_type=F32)
         return (acc[:, 0:256] + acc[:, 256:512] * (1 / 16) + acc[:, 512:768] * (1 / 256)) * unscale
 
     def first_half(t):
@@ -264,6 +267,7 @@
         near(0, p, 0, 0)
         near(0, p, 0, 1)
         near(1, p, 0, 0)
+        stage2b(p)
         home(1, p, 1)
         near2(1, p, 0)
         home(1, p, 3)
@@ -297,8 +301,19 @@
 
     for t in range(UNITS - 1):
         before(t)
-        first_half(t)
-        second_half(t)
+        if t:
+            first_half(t)
+            second_half(t)
+        else:
+            for n in range(ROWS // FIRST):
+                v, w = table(0, n, core, FIRST), table(0, n, 1 - core, FIRST)
+                if n + 1 < ROWS // FIRST:
+                    for m in range(0, FIRST, 128):
+                        split(pl.ds((n + 1) * FIRST + m, 128))
+                for c in range(2):
+                    lanes = slice(128 * c, 128 * c + 128)
+                    own[0, c] = v[:, lanes] if n == 0 else own[0, c] + v[:, lanes]
+                    part[0, c] = w[:, lanes] if n == 0 else part[0, c] + w[:, lanes]
         if t == 0:
             pl.semaphore_wait(barrier, len(peers))
         swap(t)
@@ -308,12 +323,10 @@
     w0, w1 = table(7, 0, 1 - core), table(7, 1, 1 - core)
     part[7, 0], part[7, 1] = w0[:, 0:128] + w1[:, 0:128], w0[:, 128:256] + w1[:, 128:256]
     swap(7)
-    stage2b(0)
     stage3(0)
     v0, v1 = table(7, 0, core), table(7, 1, core)
     own[7, 0], own[7, 1] = v0[:, 0:128] + v1[:, 0:128], v0[:, 128:256] + v1[:, 128:256]
 
-    stage2b(1)
     stage3(1)
 
     total = cnt_y[...]

time: 39.3 us -> 38.9 us (0.990)
  Pallas kernels: 37.4 us -> 37 us
    pallas_call x1, Pallas kernels: 37.4 us -> 37 us  [per_device(): pl.pallas_call(kernel, out_shape=(pltpu.VMEM((16, M), F32), pltpu.VMEM((1...]
where the time goes in v6:
time: 38.9 us; the launch traced here: 38.7 us
  Pallas kernels  37 us (95%)
  local copies, waits for them, and re-layouts  1.12 us (3%)
  between operations  0.64 us (2%)
    pallas_call x1, Pallas kernels, per_device(): pl.pallas_call(kernel, out_shape=(pltpu.VMEM((16, M), F32), pltpu.VMEM((1...  37 us
    unnamed x2, local copies, waits for them, and re-layouts  1.12 us

profile of v6, /device:TPU:2, one launch (start us, length us, event | category | flops | bytes accessed | tf_op | source)
XLA Modules:
  0.0 38.7 jit_solution(10257592411793414843)
XLA Ops:
  0.6 37.0 %shard_map.50 = (f32[16,256]{1,0:T(8,128)S(1)}, f32[1,16]{1,0:T(1,128)S(1)}) custom-call(s32[1,4096]{1,0:T(1,128)} %bitcast.4, s32[1,4096]{1,0:T(1,128)} %bitcast.5, f32[4096,256]{1,0:T(8,128)} %facts_ref.1), custom_call_target="tpu_custom_call" | custom-call | tf_op jit(solution)/shard_map/pallas_call | solution.py:372
  37.6 0.6 %copy.7 = f32[16,256]{1,0:T(8,128)} copy(f32[16,256]{1,0:T(8,128)S(1)} %get-tuple-element.6) | data formatting | bytes 32768
  38.2 0.5 %copy.8 = f32[16]{0:T(128)} copy(f32[16]{0:T(128)S(1)} %bitcast.3) | data formatting | bytes 128
